TPU v7x, 8 devices: a whole 2x2x1 slice. The times are simulated.
8 devices in a mesh: dp: 1 (over z), tp: 8 (over y, x, core).
Axes of the slice: x: 2, y: 2, z: 1, core: 2. Of those that a mesh axis runs over, the one named last changes fastest.
Arguments:
- x_seq: bfloat16 [3, 256, 5120], P(None, 'dp')
- cache_len: int32 [256], P('dp')
- k_cache: bfloat16 [256, 8, 256, 128], P('dp', 'tp')
- v_cache: bfloat16 [256, 8, 256, 128], P('dp', 'tp')
- w_q: bfloat16 [5120, 5120], P(None, 'tp')
- w_k: bfloat16 [5120, 1024], P(None, 'tp')
- w_v: bfloat16 [5120, 1024], P(None, 'tp')
- w_o: bfloat16 [5120, 5120], P('tp')
- w_gate: bfloat16 [5120, 27648], P(None, 'tp')
- w_up: bfloat16 [5120, 27648], P(None, 'tp')
- w_down: bfloat16 [27648, 5120], P('tp')
- g_q: bfloat16 [5120], P('tp')
- g_k: bfloat16 [1024], P('tp')
- g_attn: bfloat16 [5120], replicated
- g_mlp: bfloat16 [5120], replicated
Outputs:
- output 1: bfloat16 [3, 256, 5120], P(None, 'dp')
- output 2: bfloat16 [256, 8, 256, 128], P('dp', 'tp')
- output 3: bfloat16 [256, 8, 256, 128], P('dp', 'tp')
All inputs are finite; a program needn't handle non-finite values.
Results may differ from a plain program's by a relative error of at most 0.02.
Values are sent between devices in bfloat16 or wider.
A program may use at most 1 GiB of HBM per device.

v0:
```python
import functools

import jax
import jax.numpy as jnp
from jax import lax
from jax.experimental import pallas as pl
from jax.experimental.pallas import tpu as pltpu
from jax.sharding import PartitionSpec as P

ROPE_THETA = 500000.0
NORM_EPS = 1e-6
MESH_ID = pl.DeviceIdType.MESH
MIB = 2**20


def rms_factor(sq_sum, full_width):
    return lax.rsqrt(sq_sum / full_width + NORM_EPS)


N_KB = 5


def head_kernel(axis, q_width, kv_width, x_hbm, wq_hbm, wk_hbm, wv_hbm, gq_ref, gk_ref, len_ref, freq_ref, q_ref, kv_ref,
                xv, wv, acc, raw, sums, parts, in_sem, s_sem, r_sem):
    n_steps, n_seq, d_model = x_hbm.shape
    wq_cols = wq_hbm.shape[1]
    hd = wk_hbm.shape[1]
    n_heads = wq_cols // hd
    kw = d_model // N_KB
    n_blk = n_steps * 2
    me = lax.axis_index(axis)

    def in_copies(kb):
        ks = pl.ds(pl.multiple_of(kb * kw, kw), kw)
        return (pltpu.make_async_copy(x_hbm.at[:, :, ks], xv.at[:, :, ks], in_sem.at[kb, 0]),
                pltpu.make_async_copy(wq_hbm.at[ks, :], wv.at[ks, 0:wq_cols], in_sem.at[kb, 1]),
                pltpu.make_async_copy(wk_hbm.at[ks, :], wv.at[ks, wq_cols:wq_cols + hd], in_sem.at[kb, 2]),
                pltpu.make_async_copy(wv_hbm.at[ks, :], wv.at[ks, wq_cols + hd:wq_cols + 2 * hd], in_sem.at[kb, 3]))

    for kb in range(N_KB):
        for cp in in_copies(kb):
            cp.start()

    bar = pltpu.get_barrier_semaphore()
    for i in range(1, 8):
        pl.semaphore_signal(bar, inc=1, device_id={axis: lax.rem(me + i, 8)}, device_id_type=MESH_ID)

    def project(kb, _):
        for cp in in_copies(kb):
            cp.wait()
        ks = pl.ds(pl.multiple_of(kb * kw, kw), kw)
        for t in range(n_steps):
            part = jnp.dot(xv[t, :, ks], wv[ks, :], preferred_element_type=jnp.float32)

            @pl.when(kb == 0)
            def _():
                acc[t] = part

            @pl.when(kb > 0)
            def _():
                acc[t] += part
        return 0

    lax.fori_loop(0, N_KB, project, 0)

    lane = lax.broadcasted_iota(jnp.int32, (128, 128), 1)
    diag = lane == lax.broadcasted_iota(jnp.int32, (128, 128), 0)

    def to_row(col):
        return jnp.sum(jnp.where(diag, jnp.broadcast_to(col, (128, 128)), 0.0), axis=0, keepdims=True)

    def to_col(row):
        return jnp.sum(jnp.where(diag, jnp.broadcast_to(row, (128, 128)), 0.0), axis=1, keepdims=True)

    def rounded(v):
        return v.astype(jnp.bfloat16).astype(jnp.float32)

    sums[...] = jnp.zeros_like(sums)
    for blk in range(n_blk):
        t, half = blk // 2, blk % 2
        rows = slice(half * 128, half * 128 + 128)
        sq = None
        for g in range(n_heads):
            val = rounded(acc[t, rows, g * hd:(g + 1) * hd])
            raw[blk, g] = val
            sq = val * val if sq is None else sq + val * val
        sums[blk:blk + 1, :] = to_row(jnp.sum(sq, axis=-1, keepdims=True))
        val = rounded(acc[t, rows, wq_cols:wq_cols + hd])
        raw[blk, n_heads] = val
        sums[n_blk + blk:n_blk + blk + 1, :] = to_row(jnp.sum(val * val, axis=-1, keepdims=True))

    def exchange(i):
        return pltpu.make_async_remote_copy(src_ref=sums, dst_ref=parts.at[me], send_sem=s_sem.at[i - 1], recv_sem=r_sem.at[i - 1], device_id={axis: lax.rem(me + i, 8)}, device_id_type=MESH_ID)

    pl.semaphore_wait(bar, 7)
    for i in range(1, 8):
        exchange(i).start()
    parts[me] = sums[...]

    for blk in range(n_blk):
        t, half = blk // 2, blk % 2
        rows = slice(half * 128, half * 128 + 128)
        kv_ref[pl.ds(half * 1024 + 3 + t, 128, stride=8), :] = rounded(acc[t, rows, wq_cols + hd:wq_cols + 2 * hd])
    for half in range(2):
        zero = jnp.zeros((128, hd), jnp.float32)
        for slot in range(n_steps * n_heads, 16):
            q_ref[pl.ds(half * 2048 + slot, 128, stride=16), :] = zero
        for slot in range(2 * n_steps, 8):
            kv_ref[pl.ds(half * 1024 + slot, 128, stride=8), :] = zero
    low = lane < 64
    freq = freq_ref[...]
    lens = len_ref[...].astype(jnp.float32)
    angle = jnp.where(low, to_col(lens[0:1, :]), to_col(lens[1:2, :])) * freq
    cos_p = jnp.cos(angle)
    sin_p = jnp.sin(angle)
    cos_r = pltpu.roll(cos_p, 64, 1)
    sin_r = pltpu.roll(sin_p, 64, 1)
    cos_0 = (jnp.where(low, cos_p, cos_r), jnp.where(low, cos_r, cos_p))
    sin_0 = (jnp.where(low, sin_p, sin_r), jnp.where(low, sin_r, sin_p))

    for i in range(1, 8):
        exchange(i).wait()
    total = parts[0]
    for i in range(1, 8):
        total = total + parts[i]
    q_fac = rms_factor(total[0:n_blk], q_width)
    k_fac = rms_factor(total[n_blk:2 * n_blk], kv_width)
    gain_q = gq_ref[...].astype(jnp.float32)
    gain_k = gk_ref[...].astype(jnp.float32)

    for blk in range(n_blk):
        t, half = blk // 2, blk % 2
        if t == 0:
            cos_t, sin_t = cos_0[half], sin_0[half]
        else:
            cos_s, sin_s = jnp.cos(freq * float(t)), jnp.sin(freq * float(t))
            cos_t = cos_0[half] * cos_s - sin_0[half] * sin_s
            sin_t = sin_0[half] * cos_s + cos_0[half] * sin_s
        sin_t = jnp.where(low, -sin_t, sin_t)

        def rope(val):
            return rounded(val * cos_t + pltpu.roll(val, 64, 1) * sin_t)

        fac = to_col(q_fac[blk:blk + 1, :])
        for g in range(n_heads):
            q_ref[pl.ds(half * 2048 + t * n_heads + g, 128, stride=16), :] = rope(raw[blk, g] * fac * gain_q[:, g * hd:(g + 1) * hd])
        fac = to_col(k_fac[blk:blk + 1, :])
        kv_ref[pl.ds(half * 1024 + t, 128, stride=8), :] = rope(raw[blk, n_heads] * fac * gain_k)


def head_layer(x_seq, cache_len, w_q, w_k, w_v, g_q, g_k, q_width, kv_width, axis):
    n_steps, n_seq, d_model = x_seq.shape
    hd = w_k.shape[1]
    cols = w_q.shape[1] + 2 * hd
    half_dim = hd // 2
    bf16, f32 = jnp.bfloat16, jnp.float32
    inv_freq = ROPE_THETA ** (-(jnp.arange(half_dim, dtype=f32) * (2.0 / hd)))
    freq = jnp.concatenate([inv_freq, inv_freq]).reshape(1, hd)
    anym = pl.BlockSpec(memory_space=pl.ANY)
    vmem = pl.BlockSpec(memory_space=pltpu.VMEM)
    dma = pltpu.SemaphoreType.DMA
    return pl.pallas_call(
        functools.partial(head_kernel, axis, q_width, kv_width),
        out_shape=(jax.ShapeDtypeStruct((n_seq * 16, hd), f32), jax.ShapeDtypeStruct((n_seq * 8, hd), f32)),
        in_specs=[anym] * 4 + [vmem] * 4,
        out_specs=(vmem, vmem),
        scratch_shapes=[
            pltpu.VMEM((n_steps, n_seq, d_model), bf16),
            pltpu.VMEM((d_model, cols), bf16),
            pltpu.VMEM((n_steps, n_seq, cols), f32),
            pltpu.VMEM((2 * n_steps, w_q.shape[1] // hd + 1, 128, hd), f32),
            pltpu.VMEM((16, 128), f32),
            pltpu.VMEM((8, 16, 128), f32),
            dma((N_KB, 4)), dma((7,)), dma((7,)),
        ],
        compiler_params=pltpu.CompilerParams(collective_id=0, has_side_effects=True, vmem_limit_bytes=48 * MIB),
    )(x_seq, w_q, w_k, w_v, g_q.reshape(1, -1), g_k.reshape(1, -1), cache_len.reshape(2, n_seq // 2), freq)


SEQ_BLK = 16
SEQ_GRP = 8


def attn_kernel(n_heads, n_steps, len_ref, q_ref, kv_ref, k_ref, v_ref, o_ref, ko_ref, vo_ref):
    n_pos, hd = k_ref.shape[1:]
    fixed = n_pos // 2
    scale = hd ** -0.5
    base = pl.program_id(0) * SEQ_BLK
    row = lax.broadcasted_iota(jnp.int32, (n_pos - fixed, hd), 0)
    s_step = lax.broadcasted_iota(jnp.int32, (16, n_pos - fixed), 0) // n_heads
    s_last = lax.broadcasted_iota(jnp.int32, (16, n_pos - fixed), 1) + fixed - s_step

    def group(grp, _):
        first = grp * SEQ_GRP
        idx = [first + i for i in range(SEQ_GRP)]
        lens = [len_ref[base + i] for i in idx]
        for i, length in zip(idx, lens):
            rel = row - (length - fixed)
            for in_ref, out_ref, slot in ((k_ref, ko_ref, 0), (v_ref, vo_ref, n_steps)):
                out_ref[i, 0:fixed, :] = in_ref[i, 0:fixed, :]
                vals = in_ref[i, fixed:n_pos, :].astype(jnp.float32)
                for t in range(n_steps):
                    vals = jnp.where(rel == t, kv_ref[i, slot + t:slot + t + 1, :], vals)
                out_ref[i, fixed:n_pos, :] = vals.astype(jnp.bfloat16)
        scores = [lax.dot_general(q_ref[i].astype(jnp.bfloat16), ko_ref[i], (((1,), (1,)), ((), ())), preferred_element_type=jnp.float32) for i in idx]
        probs = []
        sums = []
        for s, length in zip(scores, lens):
            lo = s[:, 0:fixed] * scale
            hi = jnp.where(s_last <= length, s[:, fixed:n_pos] * scale, -jnp.inf)
            top = jnp.max(jnp.maximum(lo, hi), axis=-1, keepdims=True)
            lo = jnp.exp(lo - top)
            hi = jnp.exp(hi - top)
            sums.append(jnp.sum(lo + hi, axis=-1, keepdims=True))
            probs.append(jnp.concatenate([lo.astype(jnp.bfloat16), hi.astype(jnp.bfloat16)], axis=-1))
        for i, p, total in zip(idx, probs, sums):
            o_ref[i] = jnp.dot(p, vo_ref[i], preferred_element_type=jnp.float32) / total
        return 0

    lax.fori_loop(0, SEQ_BLK // SEQ_GRP, group, 0)


def attn_layer(cache_len, q, kv, k_cache, v_cache, n_heads, n_steps):
    n_seq, _, n_pos, hd = k_cache.shape
    bf16, f32 = jnp.bfloat16, jnp.float32
    cache_blk = pl.BlockSpec((SEQ_BLK, n_pos, hd), lambda i: (i, 0, 0))
    o, k_out, v_out = pl.pallas_call(
        functools.partial(attn_kernel, n_heads, n_steps),
        grid=(n_seq // SEQ_BLK,),
        out_shape=(jax.ShapeDtypeStruct((n_seq, 16, hd), f32), jax.ShapeDtypeStruct((n_seq, n_pos, hd), bf16), jax.ShapeDtypeStruct((n_seq, n_pos, hd), bf16)),
        in_specs=[pl.BlockSpec(memory_space=pltpu.SMEM), pl.BlockSpec((SEQ_BLK, 16, hd), lambda i: (i, 0, 0)), pl.BlockSpec((SEQ_BLK, 8, hd), lambda i: (i, 0, 0)), cache_blk, cache_blk],
        out_specs=(pl.BlockSpec((SEQ_BLK, 16, hd), lambda i: (i, 0, 0)), cache_blk, cache_blk),
        compiler_params=pltpu.CompilerParams(vmem_limit_bytes=48 * MIB),
    )(cache_len, q.reshape(n_seq, 16, hd), kv.reshape(n_seq, 8, hd), k_cache.reshape(n_seq, n_pos, hd), v_cache.reshape(n_seq, n_pos, hd))
    return o, k_out.reshape(k_cache.shape), v_out.reshape(v_cache.shape)


N_CB = 4
N_WB = 4
N_DB = 3
HB = 128
DB = 256


def tail_kernel(axis, o_hbm, x_hbm, wo_hbm, w1_hbm, w3_hbm, w2_hbm, ga_ref, gm_ref, y_hbm,
                on, ob, xp, hb, src, recv0, recv1, recv2, act, wob, wb, w2b,
                o_sem, x_sem, wo_sem, wb_sem, w2_sem, y_sem, s_sem, r_sem, g_ssem, g_rsem):
    n_steps, n_seq, d_model = x_hbm.shape
    half = n_seq // 2
    rows = n_steps * half
    piece = rows // 8
    cw = d_model // N_CB
    n_hid = w1_hbm.shape[1]
    n_j = n_hid // HB
    n_d = d_model // DB
    per_cb = n_d // N_CB

    me = lax.axis_index(axis)
    core = lax.rem(me, 2)
    xb = lax.rem(me // 2, 2)
    yb = me // 4
    first_bit = core * yb + (1 - core) * xb
    second_bit = core * xb + (1 - core) * yb
    fw = 1 + core
    sw = 2 - core
    partner = me + 1 - 2 * core
    fpeer = me + (1 - 2 * first_bit) * 2 * fw
    speer = me + (1 - 2 * second_bit) * 2 * sw
    fspeer = fpeer + speer - me

    def remote(src_ref, dst_ref, send, recv, dev):
        return pltpu.make_async_remote_copy(src_ref=src_ref, dst_ref=dst_ref, send_sem=send, recv_sem=recv, device_id={axis: dev}, device_id_type=MESH_ID)

    o_copy = pltpu.make_async_copy(o_hbm, on, o_sem)
    o_copy.start()

    def wo_copy(cb):
        return pltpu.make_async_copy(wo_hbm.at[:, pl.ds(cb * cw, cw)], wob.at[:, pl.ds(cb * cw, cw)], wo_sem.at[cb])

    for cb in range(N_CB):
        wo_copy(cb).start()

    def x_copy(c, i):
        r0 = piece * me + 16 * i
        t = r0 // half
        b = pl.multiple_of(lax.rem(r0, half), 16)
        return pltpu.make_async_copy(x_hbm.at[t, pl.ds(c * half + b, 16), :], xp.at[c, pl.ds(16 * i, 16), :], x_sem.at[c, i])

    for c in range(2):
        for i in range(piece // 16):
            x_copy(c, i).start()

    def wb_copies(j, s):
        col = pl.ds(pl.multiple_of(j * HB, HB), HB)
        return (pltpu.make_async_copy(w1_hbm.at[:, col], wb.at[s, :, 0:HB], wb_sem.at[s, 0]),
                pltpu.make_async_copy(w3_hbm.at[:, col], wb.at[s, :, HB:2 * HB], wb_sem.at[s, 1]))

    def w2_copy(j, s):
        return pltpu.make_async_copy(w2_hbm.at[:, pl.ds(pl.multiple_of(j * DB, DB), DB)], w2b.at[s], w2_sem.at[s])

    for s in range(N_WB - 1):
        for cp in wb_copies(s, s):
            cp.start()

    bar = pltpu.get_barrier_semaphore()
    for dev in (partner, fpeer, speer):
        pl.semaphore_signal(bar, inc=1, device_id={axis: dev}, device_id_type=MESH_ID)
    pl.semaphore_wait(bar, 3)

    def cols_of(cb):
        return pl.ds(pl.multiple_of(cb * cw, cw), cw)

    def copy0(inst, cb):
        c = inst % 2
        return remote(src.at[c, :, 1 - core, :, cols_of(cb)], recv0.at[c, :, :, cols_of(cb)], s_sem.at[inst, 0, cb], r_sem.at[inst, 0, cb], partner)

    def copy1(inst, cb, k):
        c = inst % 2
        sb = (1 - second_bit) if k == 0 else second_bit
        idx = (1 - first_bit) * fw + sb * sw
        return remote(recv0.at[c, idx, :, cols_of(cb)], recv1.at[c, k, :, cols_of(cb)], s_sem.at[inst, 1 + k, cb], r_sem.at[inst, 1 + k, cb], fpeer)

    def copy2(inst, cb):
        c = inst % 2
        return remote(recv1.at[c, 0, :, cols_of(cb)], recv2.at[c, :, cols_of(cb)], s_sem.at[inst, 3, cb], r_sem.at[inst, 3, cb], speer)

    def f32(v):
        return v.astype(jnp.float32)

    def event1(inst, cb):
        c = inst % 2
        copy0(inst, cb).wait_recv()
        cols = cols_of(cb)

        def add(i, _):
            recv0[c, i, :, cols] = (f32(src[c, i, core, :, cols]) + f32(recv0[c, i, :, cols])).astype(jnp.bfloat16)
            return 0

        lax.fori_loop(0, 4, add, 0)
        copy1(inst, cb, 0).start()
        copy1(inst, cb, 1).start()

    def event2(inst, cb):
        c = inst % 2
        copy1(inst, cb, 0).wait_recv()
        cols = cols_of(cb)
        idx = first_bit * fw + (1 - second_bit) * sw
        recv1[c, 0, :, cols] = (f32(recv0[c, idx, :, cols]) + f32(recv1[c, 0, :, cols])).astype(jnp.bfloat16)
        copy2(inst, cb).start()

    def event3(inst, cb):
        c = inst % 2
        copy1(inst, cb, 1).wait_recv()
        copy2(inst, cb).wait_recv()
        cols = cols_of(cb)
        idx = first_bit * fw + second_bit * sw
        recv2[c, :, cols] = (f32(recv0[c, idx, :, cols]) + f32(recv1[c, 1, :, cols]) + f32(recv2[c, :, cols])).astype(jnp.bfloat16)

    def rows_of(c, dev):
        return hb.at[c, pl.ds(pl.multiple_of(dev * piece, 16), piece), :]

    def gcopy(inst, k):
        c = inst % 2
        who, dev = ((me, speer), (me, fpeer), (me, partner), (speer, fpeer), (speer, partner), (fpeer, partner), (fspeer, partner))[k]
        return remote(rows_of(c, who), rows_of(c, who), g_ssem.at[inst, k], g_rsem.at[inst, k], dev)

    def event4(inst):
        c = inst % 2
        gain_ref = ga_ref if inst < 2 else gm_ref

        def one(i, _):
            r = pl.ds(pl.multiple_of(i * 16, 16), 16)
            hr = pl.ds(pl.multiple_of(me * piece + i * 16, 16), 16)
            a = f32(recv2[c, r, :])
            factor = rms_factor(jnp.sum(a * a, axis=-1, keepdims=True), d_model)
            base = f32(xp[c, r, :]) if inst < 2 else f32(hb[c, hr, :])
            hb[c, hr, :] = (base + a * factor * f32(gain_ref[...])).astype(jnp.bfloat16)
            return 0

        lax.fori_loop(0, piece // 16, one, 0)

        def drain(cb, _):
            copy0(inst, cb).wait_send()
            copy1(inst, cb, 0).wait_send()
            copy1(inst, cb, 1).wait_send()
            copy2(inst, cb).wait_send()
            return 0

        lax.fori_loop(0, N_CB, drain, 0)
        for k in (1, 0, 2):
            gcopy(inst, k).start()

    def event5(inst):
        gcopy(inst, 0).wait_recv()
        gcopy(inst, 3).start()
        gcopy(inst, 4).start()

    def event6(inst):
        gcopy(inst, 1).wait_recv()
        gcopy(inst, 5).start()

    def event7(inst):
        gcopy(inst, 3).wait_recv()
        gcopy(inst, 6).start()

    def event8(inst):
        for k in (2, 4, 5, 6):
            gcopy(inst, k).wait_recv()
        for k in range(7):
            gcopy(inst, k).wait_send()

    def span(j, start, every, fn):
        k = j - start

        @pl.when((k >= 0) & (k < every * N_CB) & (lax.rem(k + every, every) == 0))
        def _():
            fn(k // every)

    def at(j, when, fn):
        @pl.when(j == when)
        def _():
            fn()

    hd = o_hbm.shape[1]
    n_heads = wo_hbm.shape[0] // hd

    def out_proj(c):
        for t in range(n_steps):
            for g in range(n_heads):
                ob[c, t * half:(t + 1) * half, g * hd:(g + 1) * hd] = on[pl.ds(c * half * 16 + t * n_heads + g, half, stride=16), :].astype(jnp.bfloat16)

        def step(cb, _):
            part = jnp.dot(ob[c], wob[:, cols_of(cb)], preferred_element_type=jnp.float32).astype(jnp.bfloat16)
            src[c, :, :, :, cols_of(cb)] = part.reshape(4, 2, piece, cw)
            copy0(c, cb).start()
            return 0

        lax.fori_loop(0, N_CB, step, 0)

    def y_copies(c):
        return [pltpu.make_async_copy(hb.at[c, pl.ds(t * half, half), :], y_hbm.at[t, pl.ds(c * half, half), :], y_sem.at[c, t]) for t in range(n_steps)]

    o_copy.wait()
    for cb in range(N_CB):
        wo_copy(cb).wait()
    out_proj(0)
    lax.fori_loop(0, N_CB, lambda cb, _: (event1(0, cb), 0)[1], 0)
    out_proj(1)
    for c in range(2):
        for i in range(piece // 16):
            x_copy(c, i).wait()
    lax.fori_loop(0, N_CB, lambda cb, _: (event2(0, cb), 0)[1], 0)
    lax.fori_loop(0, N_CB, lambda cb, _: (event3(0, cb), 0)[1], 0)
    event4(0)
    event5(0)
    event6(0)
    event7(0)
    event8(0)

    for c in range(2):
        other = 1 + c

        def gate_up(j, _):
            s = lax.rem(j, N_WB)

            @pl.when(j + N_WB - 1 < n_j)
            def _():
                for cp in wb_copies(j + N_WB - 1, lax.rem(j + N_WB - 1, N_WB)):
                    cp.start()

            for cp in wb_copies(j, s):
                cp.wait()
            both = jnp.dot(hb[c], wb[s], preferred_element_type=jnp.float32)
            gate = both[:, :HB]
            act[:, pl.ds(pl.multiple_of(j * HB, HB), HB)] = (jax.nn.silu(gate) * both[:, HB:]).astype(jnp.bfloat16)
            span(j, 1, 1, functools.partial(event1, other))
            span(j, 6, 2, functools.partial(event2, other))
            span(j, 10, 2, functools.partial(event3, other))
            at(j, 17, functools.partial(event4, other))
            at(j, 24, functools.partial(event5, other))
            at(j, 25, functools.partial(event6, other))
            return 0

        for s in range(N_DB - 1):
            w2_copy(s, s).start()
        lax.fori_loop(0, n_j, gate_up, 0)
        if c == 0:
            for s in range(N_WB - 1):
                for cp in wb_copies(s, s):
                    cp.start()

        def down(j, _):
            s = lax.rem(j, N_DB)

            @pl.when(j + N_DB - 1 < n_d)
            def _():
                w2_copy(j + N_DB - 1, lax.rem(j + N_DB - 1, N_DB)).start()

            w2_copy(j, s).wait()
            part = jnp.dot(act[...], w2b[s], preferred_element_type=jnp.float32).astype(jnp.bfloat16)
            src[c, :, :, :, pl.ds(pl.multiple_of(j * DB, DB), DB)] = part.reshape(4, 2, piece, DB)

            @pl.when(lax.rem(j, per_cb) == per_cb - 1)
            def _():
                copy0(2 + c, j // per_cb).start()

            at(j, 7, functools.partial(event7, other))
            at(j, 10, functools.partial(event8, other))
            if c == 1:
                q = j // per_cb

                @pl.when(lax.rem(j, per_cb) == 2)
                def _():
                    @pl.when(q >= 1)
                    def _():
                        event1(3, q - 1)

                    @pl.when(q >= 2)
                    def _():
                        event2(3, q - 2)

                    @pl.when(q >= 3)
                    def _():
                        event3(3, q - 3)
            return 0

        lax.fori_loop(0, n_d, down, 0)
        if c == 1:
            for cp in y_copies(0):
                cp.start()

    event1(3, 3)
    event2(3, 2)
    event3(3, 1)
    event2(3, 3)
    event3(3, 2)
    event3(3, 3)
    event4(3)
    event5(3)
    event6(3)
    event7(3)
    event8(3)
    for cp in y_copies(1):
        cp.start()
    for c in range(2):
        for cp in y_copies(c):
            cp.wait()


def tail_layer(o, x_seq, w_o, w_gate, w_up, w_down, g_attn, g_mlp, axis):
    n_steps, n_seq, d_model = x_seq.shape
    rows = n_steps * n_seq // 2
    piece = rows // 8
    n_hid = w_gate.shape[1]
    bf16 = jnp.bfloat16
    anym = pl.BlockSpec(memory_space=pl.ANY)
    vmem = pl.BlockSpec(memory_space=pltpu.VMEM)
    dma = pltpu.SemaphoreType.DMA
    return pl.pallas_call(
        functools.partial(tail_kernel, axis),
        out_shape=jax.ShapeDtypeStruct((n_steps, n_seq, d_model), bf16),
        in_specs=[anym] * 6 + [vmem] * 2,
        out_specs=anym,
        scratch_shapes=[
            pltpu.VMEM(o.shape, jnp.float32),
            pltpu.VMEM((2, rows, w_o.shape[0]), bf16),
            pltpu.VMEM((2, piece, d_model), bf16),
            pltpu.VMEM((2, rows, d_model), bf16),
            pltpu.VMEM((2, 4, 2, piece, d_model), bf16),
            pltpu.VMEM((2, 4, piece, d_model), bf16),
            pltpu.VMEM((2, 2, piece, d_model), bf16),
            pltpu.VMEM((2, piece, d_model), bf16),
            pltpu.VMEM((rows, n_hid), bf16),
            pltpu.VMEM(w_o.shape, bf16),
            pltpu.VMEM((N_WB, d_model, 2 * HB), bf16),
            pltpu.VMEM((N_DB, n_hid, DB), bf16),
            dma, dma((2, piece // 16)), dma((N_CB,)), dma((N_WB, 2)), dma((N_DB,)), dma((2, n_steps)),
            dma((4, 4, N_CB)), dma((4, 4, N_CB)), dma((4, 7)), dma((4, 7)),
        ],
        compiler_params=pltpu.CompilerParams(collective_id=1, has_side_effects=True, vmem_limit_bytes=63 * MIB),
    )(o, x_seq, w_o, w_gate, w_up, w_down, g_attn.reshape(1, -1), g_mlp.reshape(1, -1))


def layer_steps(x_seq, cache_len, k_cache, v_cache, w_q, w_k, w_v, w_o, w_gate, w_up, w_down, g_q, g_k, g_attn, g_mlp, q_width, kv_width):
    n_steps, n_seq, _ = x_seq.shape
    hd = k_cache.shape[-1]
    q, kv = head_layer(x_seq, cache_len, w_q, w_k, w_v, g_q, g_k, q_width, kv_width, 'tp')
    o, k_out, v_out = attn_layer(cache_len, q, kv, k_cache, v_cache, w_q.shape[1] // hd, n_steps)
    y = tail_layer(o.reshape(n_seq * 16, hd), x_seq, w_o, w_gate, w_up, w_down, g_attn, g_mlp, 'tp')
    return y, k_out, v_out


def solution(mesh):
    tp_size = mesh.shape['tp']

    def local_run(x_seq, cache_len, k_cache, v_cache, w_q, w_k, w_v, w_o, w_gate, w_up, w_down, g_q, g_k, g_attn, g_mlp):
        return layer_steps(x_seq, cache_len, k_cache, v_cache, w_q, w_k, w_v, w_o, w_gate, w_up, w_down, g_q, g_k, g_attn, g_mlp, w_q.shape[1] * tp_size, w_k.shape[1] * tp_size)

    data_spec = P(None, 'dp', None)
    cache_spec = P('dp', 'tp', None, None)
    col_spec = P(None, 'tp')
    row_spec = P('tp', None)
    arg_specs = (data_spec, P('dp'), cache_spec, cache_spec, col_spec, col_spec, col_spec, row_spec, col_spec, col_spec, row_spec, P('tp'), P('tp'), P(None), P(None))
    out_specs = (data_spec, cache_spec, cache_spec)
    return jax.shard_map(local_run, mesh=mesh, in_specs=arg_specs, out_specs=out_specs, check_vma=False)
```

profile of v0, /device:TPU:0, one launch (start us, length us, event | category | flops | bytes accessed | tf_op | source)
XLA Modules:
  0.0 276.4 jit_solution(12130891793145040375)
XLA Ops:
  0.6 0.1 maximum_bitcast_fusion.freq_ref
  0.7 0.7 reshape.45.gq_ref
  1.4 1.3 reshape.54.ga_ref
  2.7 1.3 reshape.55.gm_ref
  4.0 0.0 copy-start.1
  4.0 1.3 copy-done.1
  5.4 0.0 copy-start.2
  5.4 1.3 copy-done.2
  6.7 0.0 copy-start.3
  6.7 0.7 copy-done.3
  7.4 0.0 copy-start.4
  7.4 0.7 copy-done.4
  8.0 22.5 %shard_map.166 = (f32[4096,128]{1,0:T(8,128)S(1)}, f32[2048,128]{1,0:T(8,128)S(1)}) custom-call(bf16[3,256,5120]{2,1,0:T(8,128)(2,1)} %x_hbm.3, bf16[5120,640]{1,0:T(8,128)(2,1)} %wq_hbm.1, bf16[5120,128]{1,0:T(8,128)(2,1)S(1)} %copy-done.1, bf16[5120,128]{1,0:T(8,128)(2,1)S(1)} %copy-done.2, bf16[1,640]{1,0:T(2,128)(2,1)S(1)} %reshape.45.gq_ref, ...), custom_call_target="tpu_custom_call" | custom-call | tf_op jit(solution)/shard_map/pallas_call | solution.py:162
  30.6 33.0 %shard_map.167 = (f32[256,16,128]{2,1,0:T(8,128)S(1)}, bf16[256,256,128]{2,1,0:T(8,128)(2,1)}, bf16[256,256,128]{2,1,0:T(8,128)(2,1)}) custom-call(s32[256]{0:T(256)S(1)} %copy-done.3, f32[256,16,128]{2,1,0:T(8,128)S(1)} %bitcast.16, f32[256,8,128]{2,1,0:T(8,128)S(1)} %bitcast.17, bf16[256,256,128]{2,1,0:T(8,128)(2,1)} %bitcast.20, ...), custom_call_target="tpu_custom_call" | custom-call | tf_op jit(solution)/shard_map/pallas_call | solution.py:227
  63.6 0.0 copy-start
  63.6 1.3 copy-done
  64.9 204.5 %shard_map.168 = bf16[3,256,5120]{2,1,0:T(8,128)(2,1)} custom-call(f32[4096,128]{1,0:T(8,128)} %bitcast.15, bf16[3,256,5120]{2,1,0:T(8,128)(2,1)} %x_hbm.3, bf16[640,5120]{1,0:T(8,128)(2,1)} %wo_hbm.1, bf16[5120,3456]{1,0:T(8,128)(2,1)} %w1_hbm.1, bf16[5120,3456]{1,0:T(8,128)(2,1)} %w3_hbm.1, bf16[3456,5120]{1,0:T(8,128)(2,1)} %w2_hbm.1, ...), custom_call_target="tpu_custom_call" | custom-call | tf_op jit(solution)/shard_map/pallas_call | solution.py:559
  269.4 7.0 %copy.21 = bf16[3,256,5120]{2,1,0:T(8,128)(2,1)} copy(bf16[3,256,5120]{2,1,0:T(8,128)(2,1)} %shard_map.168) | data formatting | bytes 15728640
  (1 shorter events, 0.0 us)
Async XLA Ops:
  4.0 1.3 copy-start.1
  5.4 1.3 copy-start.2
  6.7 0.7 copy-start.3
  7.4 0.7 copy-start.4
  63.6 1.3 copy-start
where the time goes:
time: 277 us; the launch traced here: 276 us
  Pallas kernels  260 us (94%)
  local copies, waits for them, and re-layouts  15.6 us (6%)
    pallas_call x1, Pallas kernels, tail_layer(): pl.pallas_call(functools.partial(tail_kernel, axis), out_shape=jax.ShapeD...  204 us
    pallas_call x1, Pallas kernels, attn_layer(): pl.pallas_call(functools.partial(attn_kernel, n_heads, n_steps), grid=(n_...  33 us
    pallas_call x1, Pallas kernels, head_layer(): pl.pallas_call(functools.partial(head_kernel, axis, q_width, kv_width), o...  22.5 us
    unnamed x11, local copies, waits for them, and re-layouts  12.3 us

commit v1 on v0

--- a/solution.py
+++ b/solution.py
@@ -235,25 +235,27 @@
     return o, k_out.reshape(k_cache.shape), v_out.reshape(v_cache.shape)
 
 
-N_CB = 4
+N_CB = 5
+N_SUB = 2
 N_WB = 4
 N_DB = 3
 HB = 128
-DB = 256
-
-
-def tail_kernel(axis, o_hbm, x_hbm, wo_hbm, w1_hbm, w3_hbm, w2_hbm, ga_ref, gm_ref, y_hbm,
-                on, ob, xp, hb, src, recv0, recv1, recv2, act, wob, wb, w2b,
-                o_sem, x_sem, wo_sem, wb_sem, w2_sem, y_sem, s_sem, r_sem, g_ssem, g_rsem):
+DB = 512
+
+
+def tail_kernel(axis, o_hbm, x_hbm, wo_hbm, w1_hbm, w3_hbm, w2_hbm, gains_hbm, y_hbm,
+                on, ob, xp, hb, src, recv0, recv1, recv2, act, wob, wb, w2b, gains,
+                o_sem, x_sem, wo_sem, wb_sem, w2_sem, y_sem, gain_sem, s_sem, r_sem, g_ssem, g_rsem):
     n_steps, n_seq, d_model = x_hbm.shape
-    half = n_seq // 2
-    rows = n_steps * half
-    piece = rows // 8
+    piece = n_seq // 8
+    sub_rows = piece // N_SUB
     cw = d_model // N_CB
     n_hid = w1_hbm.shape[1]
     n_j = n_hid // HB
     n_d = d_model // DB
     per_cb = n_d // N_CB
+    hd = o_hbm.shape[1]
+    n_heads = wo_hbm.shape[0] // hd
 
     me = lax.axis_index(axis)
     core = lax.rem(me, 2)
@@ -279,16 +281,10 @@
 
     for cb in range(N_CB):
         wo_copy(cb).start()
-
-    def x_copy(c, i):
-        r0 = piece * me + 16 * i
-        t = r0 // half
-        b = pl.multiple_of(lax.rem(r0, half), 16)
-        return pltpu.make_async_copy(x_hbm.at[t, pl.ds(c * half + b, 16), :], xp.at[c, pl.ds(16 * i, 16), :], x_sem.at[c, i])
-
-    for c in range(2):
-        for i in range(piece // 16):
-            x_copy(c, i).start()
+    gain_copy = pltpu.make_async_copy(gains_hbm, gains, gain_sem)
+    gain_copy.start()
+    x_copy = pltpu.make_async_copy(x_hbm.at[:, pl.ds(pl.multiple_of(piece * me, piece), piece), :], xp, x_sem)
+    x_copy.start()
 
     def wb_copies(j, s):
         col = pl.ds(pl.multiple_of(j * HB, HB), HB)
@@ -298,9 +294,12 @@
     def w2_copy(j, s):
         return pltpu.make_async_copy(w2_hbm.at[:, pl.ds(pl.multiple_of(j * DB, DB), DB)], w2b.at[s], w2_sem.at[s])
 
-    for s in range(N_WB - 1):
-        for cp in wb_copies(s, s):
-            cp.start()
+    def start_wb():
+        for s in range(N_WB - 1):
+            for cp in wb_copies(s, s):
+                cp.start()
+
+    start_wb()
 
     bar = pltpu.get_barrier_semaphore()
     for dev in (partner, fpeer, speer):
@@ -311,24 +310,24 @@
         return pl.ds(pl.multiple_of(cb * cw, cw), cw)
 
     def copy0(inst, cb):
-        c = inst % 2
+        c = inst % n_steps
         return remote(src.at[c, :, 1 - core, :, cols_of(cb)], recv0.at[c, :, :, cols_of(cb)], s_sem.at[inst, 0, cb], r_sem.at[inst, 0, cb], partner)
 
     def copy1(inst, cb, k):
-        c = inst % 2
+        c = inst % n_steps
         sb = (1 - second_bit) if k == 0 else second_bit
         idx = (1 - first_bit) * fw + sb * sw
         return remote(recv0.at[c, idx, :, cols_of(cb)], recv1.at[c, k, :, cols_of(cb)], s_sem.at[inst, 1 + k, cb], r_sem.at[inst, 1 + k, cb], fpeer)
 
     def copy2(inst, cb):
-        c = inst % 2
+        c = inst % n_steps
         return remote(recv1.at[c, 0, :, cols_of(cb)], recv2.at[c, :, cols_of(cb)], s_sem.at[inst, 3, cb], r_sem.at[inst, 3, cb], speer)
 
     def f32(v):
         return v.astype(jnp.float32)
 
     def event1(inst, cb):
-        c = inst % 2
+        c = inst % n_steps
         copy0(inst, cb).wait_recv()
         cols = cols_of(cb)
 
@@ -341,7 +340,7 @@
         copy1(inst, cb, 1).start()
 
     def event2(inst, cb):
-        c = inst % 2
+        c = inst % n_steps
         copy1(inst, cb, 0).wait_recv()
         cols = cols_of(cb)
         idx = first_bit * fw + (1 - second_bit) * sw
@@ -349,118 +348,132 @@
         copy2(inst, cb).start()
 
     def event3(inst, cb):
-        c = inst % 2
+        c = inst % n_steps
         copy1(inst, cb, 1).wait_recv()
         copy2(inst, cb).wait_recv()
         cols = cols_of(cb)
         idx = first_bit * fw + second_bit * sw
         recv2[c, :, cols] = (f32(recv0[c, idx, :, cols]) + f32(recv1[c, 1, :, cols]) + f32(recv2[c, :, cols])).astype(jnp.bfloat16)
 
-    def rows_of(c, dev):
-        return hb.at[c, pl.ds(pl.multiple_of(dev * piece, 16), piece), :]
-
-    def gcopy(inst, k):
-        c = inst % 2
+    def gcopy(inst, k, sub):
+        c = inst % n_steps
         who, dev = ((me, speer), (me, fpeer), (me, partner), (speer, fpeer), (speer, partner), (fpeer, partner), (fspeer, partner))[k]
-        return remote(rows_of(c, who), rows_of(c, who), g_ssem.at[inst, k], g_rsem.at[inst, k], dev)
-
-    def event4(inst):
-        c = inst % 2
-        gain_ref = ga_ref if inst < 2 else gm_ref
-
-        def one(i, _):
-            r = pl.ds(pl.multiple_of(i * 16, 16), 16)
-            hr = pl.ds(pl.multiple_of(me * piece + i * 16, 16), 16)
-            a = f32(recv2[c, r, :])
-            factor = rms_factor(jnp.sum(a * a, axis=-1, keepdims=True), d_model)
-            base = f32(xp[c, r, :]) if inst < 2 else f32(hb[c, hr, :])
-            hb[c, hr, :] = (base + a * factor * f32(gain_ref[...])).astype(jnp.bfloat16)
-            return 0
-
-        lax.fori_loop(0, piece // 16, one, 0)
-
-        def drain(cb, _):
-            copy0(inst, cb).wait_send()
-            copy1(inst, cb, 0).wait_send()
-            copy1(inst, cb, 1).wait_send()
-            copy2(inst, cb).wait_send()
-            return 0
-
-        lax.fori_loop(0, N_CB, drain, 0)
+        part = hb.at[c, pl.ds(pl.multiple_of(who * piece + sub * sub_rows, sub_rows), sub_rows), :]
+        return remote(part, part, g_ssem.at[inst, k, sub], g_rsem.at[inst, k, sub], dev)
+
+    def event4(inst, sub):
+        c = inst % n_steps
+        attn = inst < n_steps
+
+        @pl.when(sub == 0)
+        def _():
+            def drain(cb, _):
+                copy0(inst, cb).wait_send()
+                copy1(inst, cb, 0).wait_send()
+                copy1(inst, cb, 1).wait_send()
+                copy2(inst, cb).wait_send()
+                return 0
+
+            lax.fori_loop(0, N_CB, drain, 0)
+
+        r = pl.ds(pl.multiple_of(sub * sub_rows, sub_rows), sub_rows)
+        hr = pl.ds(pl.multiple_of(me * piece + sub * sub_rows, sub_rows), sub_rows)
+        a = f32(recv2[c, r, :])
+        factor = rms_factor(jnp.sum(a * a, axis=-1, keepdims=True), d_model)
+        base = f32(xp[c, r, :]) if attn else f32(hb[c, hr, :])
+        gain = gains[0:1, :] if attn else gains[1:2, :]
+        hb[c, hr, :] = (base + a * factor * gain).astype(jnp.bfloat16)
         for k in (1, 0, 2):
-            gcopy(inst, k).start()
-
-    def event5(inst):
-        gcopy(inst, 0).wait_recv()
-        gcopy(inst, 3).start()
-        gcopy(inst, 4).start()
-
-    def event6(inst):
-        gcopy(inst, 1).wait_recv()
-        gcopy(inst, 5).start()
-
-    def event7(inst):
-        gcopy(inst, 3).wait_recv()
-        gcopy(inst, 6).start()
-
-    def event8(inst):
+            gcopy(inst, k, sub).start()
+
+    def event5(inst, sub):
+        gcopy(inst, 0, sub).wait_recv()
+        gcopy(inst, 3, sub).start()
+        gcopy(inst, 4, sub).start()
+        gcopy(inst, 1, sub).wait_recv()
+        gcopy(inst, 5, sub).start()
+
+    def event7(inst, sub):
+        gcopy(inst, 3, sub).wait_recv()
+        gcopy(inst, 6, sub).start()
+
+    def event8(inst, sub):
         for k in (2, 4, 5, 6):
-            gcopy(inst, k).wait_recv()
+            gcopy(inst, k, sub).wait_recv()
         for k in range(7):
-            gcopy(inst, k).wait_send()
-
-    def span(j, start, every, fn):
-        k = j - start
-
-        @pl.when((k >= 0) & (k < every * N_CB) & (lax.rem(k + every, every) == 0))
-        def _():
-            fn(k // every)
-
-    def at(j, when, fn):
-        @pl.when(j == when)
-        def _():
-            fn()
-
-    hd = o_hbm.shape[1]
-    n_heads = wo_hbm.shape[0] // hd
+            gcopy(inst, k, sub).wait_send()
+
+    def run(j, table):
+        for event, inst, start, every, count in table:
+            k = j - start
+            cond = (k >= 0) & (k < every * count)
+            if every > 1:
+                cond = cond & (lax.rem(k, every) == 0)
+
+            @pl.when(cond)
+            def _():
+                event(inst, k // every)
+
+    def loop(n, fn):
+        lax.fori_loop(0, n, lambda i, _: (fn(i), 0)[1], 0)
 
     def out_proj(c):
-        for t in range(n_steps):
-            for g in range(n_heads):
-                ob[c, t * half:(t + 1) * half, g * hd:(g + 1) * hd] = on[pl.ds(c * half * 16 + t * n_heads + g, half, stride=16), :].astype(jnp.bfloat16)
-
-        def step(cb, _):
-            part = jnp.dot(ob[c], wob[:, cols_of(cb)], preferred_element_type=jnp.float32).astype(jnp.bfloat16)
+        for g in range(n_heads):
+            ob[:, g * hd:(g + 1) * hd] = on[pl.ds(c * n_heads + g, n_seq, stride=16), :].astype(jnp.bfloat16)
+
+        def step(cb):
+            part = jnp.dot(ob[...], wob[:, cols_of(cb)], preferred_element_type=jnp.float32).astype(jnp.bfloat16)
             src[c, :, :, :, cols_of(cb)] = part.reshape(4, 2, piece, cw)
             copy0(c, cb).start()
-            return 0
-
-        lax.fori_loop(0, N_CB, step, 0)
-
-    def y_copies(c):
-        return [pltpu.make_async_copy(hb.at[c, pl.ds(t * half, half), :], y_hbm.at[t, pl.ds(c * half, half), :], y_sem.at[c, t]) for t in range(n_steps)]
+
+        loop(N_CB, step)
+
+    def y_copy(c):
+        return pltpu.make_async_copy(hb.at[c], y_hbm.at[c], y_sem.at[c])
 
     o_copy.wait()
     for cb in range(N_CB):
         wo_copy(cb).wait()
     out_proj(0)
-    lax.fori_loop(0, N_CB, lambda cb, _: (event1(0, cb), 0)[1], 0)
+    loop(N_CB, functools.partial(event1, 0))
     out_proj(1)
-    for c in range(2):
-        for i in range(piece // 16):
-            x_copy(c, i).wait()
-    lax.fori_loop(0, N_CB, lambda cb, _: (event2(0, cb), 0)[1], 0)
-    lax.fori_loop(0, N_CB, lambda cb, _: (event3(0, cb), 0)[1], 0)
-    event4(0)
-    event5(0)
-    event6(0)
-    event7(0)
-    event8(0)
-
-    for c in range(2):
-        other = 1 + c
-
-        def gate_up(j, _):
+    out_proj(2)
+    x_copy.wait()
+    gain_copy.wait()
+
+    def finish_reduce(inst):
+        def step(k):
+            @pl.when(k < N_CB)
+            def _():
+                event2(inst, k)
+
+            @pl.when(k > 0)
+            def _():
+                event3(inst, k - 1)
+
+        loop(N_CB + 1, step)
+
+    def finish_gather(inst):
+        loop(N_SUB, functools.partial(event4, inst))
+        loop(N_SUB, functools.partial(event5, inst))
+        loop(N_SUB, functools.partial(event7, inst))
+        loop(N_SUB, functools.partial(event8, inst))
+
+    finish_reduce(0)
+    finish_gather(0)
+
+    gate_tables = (
+        ((event1, 1, 0, 1, N_CB), (event2, 1, 4, 2, N_CB), (event3, 1, 9, 2, N_CB), (event4, 1, 18, 1, N_SUB), (event1, 2, 20, 1, N_CB)),
+        ((event1, 3, 0, 1, N_CB), (event2, 3, 6, 3, N_CB), (event5, 2, 10, 1, N_SUB), (event3, 3, 10, 3, N_CB), (event7, 2, 17, 1, N_SUB), (event8, 2, 20, 1, N_SUB), (event4, 3, 24, 1, N_SUB)),
+        ((event1, 4, 0, 1, N_CB), (event7, 3, 2, 1, N_SUB), (event2, 4, 6, 2, N_CB), (event8, 3, 7, 1, N_SUB), (event3, 4, 10, 2, N_CB), (event4, 4, 19, 1, N_SUB)),
+    )
+    down_tables = (
+        ((event2, 2, 0, 1, N_CB), (event3, 2, 4, 1, N_CB), (event5, 1, 3, 1, N_SUB), (event7, 1, 7, 1, N_SUB), (event8, 1, 9, 1, 1)),
+        ((event5, 3, 6, 1, N_SUB),),
+        ((event5, 4, 3, 1, N_SUB), (event7, 4, 6, 1, N_SUB), (event8, 4, 8, 1, N_SUB)),
+    )
+    for c in range(n_steps):
+        def gate_up(j):
             s = lax.rem(j, N_WB)
 
             @pl.when(j + N_WB - 1 < n_j)
@@ -473,23 +486,9 @@
             both = jnp.dot(hb[c], wb[s], preferred_element_type=jnp.float32)
             gate = both[:, :HB]
             act[:, pl.ds(pl.multiple_of(j * HB, HB), HB)] = (jax.nn.silu(gate) * both[:, HB:]).astype(jnp.bfloat16)
-            span(j, 1, 1, functools.partial(event1, other))
-            span(j, 6, 2, functools.partial(event2, other))
-            span(j, 10, 2, functools.partial(event3, other))
-            at(j, 17, functools.partial(event4, other))
-            at(j, 24, functools.partial(event5, other))
-            at(j, 25, functools.partial(event6, other))
-            return 0
-
-        for s in range(N_DB - 1):
-            w2_copy(s, s).start()
-        lax.fori_loop(0, n_j, gate_up, 0)
-        if c == 0:
-            for s in range(N_WB - 1):
-                for cp in wb_copies(s, s):
-                    cp.start()
-
-        def down(j, _):
+            run(j, gate_tables[c])
+
+        def down(j):
             s = lax.rem(j, N_DB)
 
             @pl.when(j + N_DB - 1 < n_d)
@@ -502,83 +501,71 @@
 
             @pl.when(lax.rem(j, per_cb) == per_cb - 1)
             def _():
-                copy0(2 + c, j // per_cb).start()
-
-            at(j, 7, functools.partial(event7, other))
-            at(j, 10, functools.partial(event8, other))
-            if c == 1:
-                q = j // per_cb
-
-                @pl.when(lax.rem(j, per_cb) == 2)
-                def _():
-                    @pl.when(q >= 1)
-                    def _():
-                        event1(3, q - 1)
-
-                    @pl.when(q >= 2)
-                    def _():
-                        event2(3, q - 2)
-
-                    @pl.when(q >= 3)
-                    def _():
-                        event3(3, q - 3)
-            return 0
-
-        lax.fori_loop(0, n_d, down, 0)
-        if c == 1:
-            for cp in y_copies(0):
-                cp.start()
-
-    event1(3, 3)
-    event2(3, 2)
-    event3(3, 1)
-    event2(3, 3)
-    event3(3, 2)
-    event3(3, 3)
-    event4(3)
-    event5(3)
-    event6(3)
-    event7(3)
-    event8(3)
-    for cp in y_copies(1):
-        cp.start()
-    for c in range(2):
-        for cp in y_copies(c):
-            cp.wait()
+                copy0(n_steps + c, j // per_cb).start()
+
+            run(j, down_tables[c])
+            if c == n_steps - 1:
+                run(j, ((event1, n_steps + c, 2, 2, 4), (event2, n_steps + c, 5, 2, 3), (event3, n_steps + c, 8, 2, 1)))
+
+        for s in range(N_DB - 1):
+            w2_copy(s, s).start()
+        loop(n_j, gate_up)
+        if c < n_steps - 1:
+            start_wb()
+        loop(n_d, down)
+        if c == 0:
+            event8(1, 1)
+            event4(2, 0)
+            event4(2, 1)
+
+    last = 2 * n_steps - 1
+    for c in range(n_steps - 1):
+        y_copy(c).start()
+    event1(last, 4)
+    event2(last, 3)
+    event3(last, 1)
+    event3(last, 2)
+    event2(last, 4)
+    event3(last, 3)
+    event3(last, 4)
+    finish_gather(last)
+    y_copy(n_steps - 1).start()
+    for c in range(n_steps):
+        y_copy(c).wait()
 
 
 def tail_layer(o, x_seq, w_o, w_gate, w_up, w_down, g_attn, g_mlp, axis):
     n_steps, n_seq, d_model = x_seq.shape
-    rows = n_steps * n_seq // 2
-    piece = rows // 8
+    piece = n_seq // 8
     n_hid = w_gate.shape[1]
     bf16 = jnp.bfloat16
     anym = pl.BlockSpec(memory_space=pl.ANY)
-    vmem = pl.BlockSpec(memory_space=pltpu.VMEM)
     dma = pltpu.SemaphoreType.DMA
+    gains = jnp.stack([g_attn, g_mlp]).astype(jnp.float32)
     return pl.pallas_call(
         functools.partial(tail_kernel, axis),
         out_shape=jax.ShapeDtypeStruct((n_steps, n_seq, d_model), bf16),
-        in_specs=[anym] * 6 + [vmem] * 2,
+        in_specs=[anym] * 7,
         out_specs=anym,
         scratch_shapes=[
             pltpu.VMEM(o.shape, jnp.float32),
-            pltpu.VMEM((2, rows, w_o.shape[0]), bf16),
-            pltpu.VMEM((2, piece, d_model), bf16),
-            pltpu.VMEM((2, rows, d_model), bf16),
-            pltpu.VMEM((2, 4, 2, piece, d_model), bf16),
-            pltpu.VMEM((2, 4, piece, d_model), bf16),
-            pltpu.VMEM((2, 2, piece, d_model), bf16),
-            pltpu.VMEM((2, piece, d_model), bf16),
-            pltpu.VMEM((rows, n_hid), bf16),
+            pltpu.VMEM((n_seq, w_o.shape[0]), bf16),
+            pltpu.VMEM((n_steps, piece, d_model), bf16),
+            pltpu.VMEM((n_steps, n_seq, d_model), bf16),
+            pltpu.VMEM((n_steps, 4, 2, piece, d_model), bf16),
+            pltpu.VMEM((n_steps, 4, piece, d_model), bf16),
+            pltpu.VMEM((n_steps, 2, piece, d_model), bf16),
+            pltpu.VMEM((n_steps, piece, d_model), bf16),
+            pltpu.VMEM((n_seq, n_hid), bf16),
             pltpu.VMEM(w_o.shape, bf16),
             pltpu.VMEM((N_WB, d_model, 2 * HB), bf16),
             pltpu.VMEM((N_DB, n_hid, DB), bf16),
-            dma, dma((2, piece // 16)), dma((N_CB,)), dma((N_WB, 2)), dma((N_DB,)), dma((2, n_steps)),
-            dma((4, 4, N_CB)), dma((4, 4, N_CB)), dma((4, 7)), dma((4, 7)),
+            pltpu.VMEM((2, d_model), jnp.float32),
+            dma, dma, dma((N_CB,)), dma((N_WB, 2)), dma((N_DB,)), dma((n_steps,)), dma,
+            dma((2 * n_steps, 4, N_CB)), dma((2 * n_steps, 4, N_CB)), dma((2 * n_steps, 7, N_SUB)), dma((2 * n_steps, 7, N_SUB)),
         ],
         compiler_params=pltpu.CompilerParams(collective_id=1, has_side_effects=True, vmem_limit_bytes=63 * MIB),
-    )(o, x_seq, w_o, w_gate, w_up, w_down, g_attn.reshape(1, -1), g_mlp.reshape(1, -1))
+    )(o, x_seq, w_o, w_gate, w_up, w_down, gains)
 
 
 def layer_steps(x_seq, cache_len, k_cache, v_cache, w_q, w_k, w_v, w_o, w_gate, w_up, w_down, g_q, g_k, g_attn, g_mlp, q_width, kv_width):

time: 277 us -> 271 us (0.978)
  Pallas kernels: 260 us -> 255 us
    pallas_call x1, Pallas kernels: 204 us -> 199 us  [tail_layer(): pl.pallas_call(functools.partial(tail_kernel, axis), out_shape=jax.ShapeD...]
where the time goes in v1:
time: 271 us
  Pallas kernels  255 us (94%)
  local copies, waits for them, and re-layouts  14.4 us (5%)
    pallas_call x1, Pallas kernels, tail_layer(): pl.pallas_call(functools.partial(tail_kernel, axis), out_shape=jax.ShapeD...  199 us
    pallas_call x1, Pallas kernels, attn_layer(): pl.pallas_call(functools.partial(attn_kernel, n_heads, n_steps), grid=(n_...  33 us
    pallas_call x1, Pallas kernels, head_layer(): pl.pallas_call(functools.partial(head_kernel, axis, q_width, kv_width), o...  22.5 us
    unnamed x11, local copies, waits for them, and re-layouts  12.3 us

profile of v1, /device:TPU:0, one launch (start us, length us, event | category | flops | bytes accessed | tf_op | source)
XLA Modules:
  0.0 270.6 jit_solution(17018652264684570901)
XLA Ops:
  0.6 0.1 maximum_bitcast_fusion.freq_ref
  0.7 0.7 reshape.39.gq_ref
  1.4 0.7 stack.9
  2.1 0.7 stack.10
  2.8 0.7 maximum_convert_fusion.gains_hbm
  3.5 0.0 copy-start.1
  3.5 1.3 copy-done.1
  4.8 0.0 copy-start.2
  4.8 1.3 copy-done.2
  6.1 0.0 copy-start.3
  6.2 0.7 copy-done.3
  6.8 0.0 copy-start.4
  6.8 0.7 copy-done.4
  7.5 22.5 %shard_map.166 = (f32[4096,128]{1,0:T(8,128)S(1)}, f32[2048,128]{1,0:T(8,128)S(1)}) custom-call(bf16[3,256,5120]{2,1,0:T(8,128)(2,1)} %x_hbm.3, bf16[5120,640]{1,0:T(8,128)(2,1)} %wq_hbm.1, bf16[5120,128]{1,0:T(8,128)(2,1)S(1)} %copy-done.1, bf16[5120,128]{1,0:T(8,128)(2,1)S(1)} %copy-done.2, bf16[1,640]{1,0:T(2,128)(2,1)S(1)} %reshape.39.gq_ref, ...), custom_call_target="tpu_custom_call" | custom-call | tf_op jit(solution)/shard_map/pallas_call | solution.py:162
  30.0 33.0 %shard_map.167 = (f32[256,16,128]{2,1,0:T(8,128)S(1)}, bf16[256,256,128]{2,1,0:T(8,128)(2,1)}, bf16[256,256,128]{2,1,0:T(8,128)(2,1)}) custom-call(s32[256]{0:T(256)S(1)} %copy-done.3, f32[256,16,128]{2,1,0:T(8,128)S(1)} %bitcast.16, f32[256,8,128]{2,1,0:T(8,128)S(1)} %bitcast.17, bf16[256,256,128]{2,1,0:T(8,128)(2,1)} %bitcast.20, ...), custom_call_target="tpu_custom_call" | custom-call | tf_op jit(solution)/shard_map/pallas_call | solution.py:227
  63.1 0.0 copy-start
  63.1 1.3 copy-done
  64.4 199.2 %shard_map.168 = bf16[3,256,5120]{2,1,0:T(8,128)(2,1)} custom-call(f32[4096,128]{1,0:T(8,128)} %bitcast.15, bf16[3,256,5120]{2,1,0:T(8,128)(2,1)} %x_hbm.3, bf16[640,5120]{1,0:T(8,128)(2,1)} %wo_hbm.1, bf16[5120,3456]{1,0:T(8,128)(2,1)} %w1_hbm.1, bf16[5120,3456]{1,0:T(8,128)(2,1)} %w3_hbm.1, bf16[3456,5120]{1,0:T(8,128)(2,1)} %w2_hbm.1, ...), custom_call_target="tpu_custom_call" | custom-call | tf_op jit(solution)/shard_map/pallas_call | solution.py:545
  263.6 7.0 %copy.21 = bf16[3,256,5120]{2,1,0:T(8,128)(2,1)} copy(bf16[3,256,5120]{2,1,0:T(8,128)(2,1)} %shard_map.168) | data formatting | bytes 15728640
  (1 shorter events, 0.0 us)
Async XLA Ops:
  3.5 1.3 copy-start.1
  4.8 1.3 copy-start.2
  6.1 0.7 copy-start.3
  6.8 0.7 copy-start.4
  63.1 1.3 copy-start

commit v2 on v1

--- a/solution.py
+++ b/solution.py
@@ -20,8 +20,8 @@
 N_KB = 5
 
 
-def head_kernel(axis, q_width, kv_width, x_hbm, wq_hbm, wk_hbm, wv_hbm, gq_ref, gk_ref, len_ref, freq_ref, q_ref, kv_ref,
-                xv, wv, acc, raw, sums, parts, in_sem, s_sem, r_sem):
+def head_kernel(axis, q_width, kv_width, x_hbm, wq_hbm, wk_hbm, wv_hbm, gq_hbm, gk_hbm, len_hbm, freq_hbm, q_ref, kv_ref,
+                xv, wv, acc, raw, sums, parts, gq_ref, gk_ref, len_ref, freq_ref, in_sem, small_sem, s_sem, r_sem):
     n_steps, n_seq, d_model = x_hbm.shape
     wq_cols = wq_hbm.shape[1]
     hd = wk_hbm.shape[1]
@@ -41,6 +41,10 @@
         for cp in in_copies(kb):
             cp.start()
 
+    small = [pltpu.make_async_copy(hbm, vmem, small_sem.at[n]) for n, (hbm, vmem) in enumerate(((gq_hbm, gq_ref), (gk_hbm, gk_ref), (len_hbm, len_ref), (freq_hbm, freq_ref)))]
+    for cp in small:
+        cp.start()
+
     bar = pltpu.get_barrier_semaphore()
     for i in range(1, 8):
         pl.semaphore_signal(bar, inc=1, device_id={axis: lax.rem(me + i, 8)}, device_id_type=MESH_ID)
@@ -50,17 +54,10 @@
             cp.wait()
         ks = pl.ds(pl.multiple_of(kb * kw, kw), kw)
         for t in range(n_steps):
-            part = jnp.dot(xv[t, :, ks], wv[ks, :], preferred_element_type=jnp.float32)
-
-            @pl.when(kb == 0)
-            def _():
-                acc[t] = part
-
-            @pl.when(kb > 0)
-            def _():
-                acc[t] += part
+            acc[t] += jnp.dot(xv[t, :, ks], wv[ks, :], preferred_element_type=jnp.float32)
         return 0
 
+    acc[...] = jnp.zeros_like(acc)
     lax.fori_loop(0, N_KB, project, 0)
 
     lane = lax.broadcasted_iota(jnp.int32, (128, 128), 1)
@@ -107,6 +104,8 @@
             q_ref[pl.ds(half * 2048 + slot, 128, stride=16), :] = zero
         for slot in range(2 * n_steps, 8):
             kv_ref[pl.ds(half * 1024 + slot, 128, stride=8), :] = zero
+    for cp in small:
+        cp.wait()
     low = lane < 64
     freq = freq_ref[...]
     lens = len_ref[...].astype(jnp.float32)
@@ -125,8 +124,8 @@
         total = total + parts[i]
     q_fac = rms_factor(total[0:n_blk], q_width)
     k_fac = rms_factor(total[n_blk:2 * n_blk], kv_width)
-    gain_q = gq_ref[...].astype(jnp.float32)
-    gain_k = gk_ref[...].astype(jnp.float32)
+    gain_q = gq_ref[...].astype(jnp.float32).reshape(1, wq_cols)
+    gain_k = gk_ref[...].astype(jnp.float32).reshape(1, hd)
 
     for blk in range(n_blk):
         t, half = blk // 2, blk % 2
@@ -162,7 +161,7 @@
     return pl.pallas_call(
         functools.partial(head_kernel, axis, q_width, kv_width),
         out_shape=(jax.ShapeDtypeStruct((n_seq * 16, hd), f32), jax.ShapeDtypeStruct((n_seq * 8, hd), f32)),
-        in_specs=[anym] * 4 + [vmem] * 4,
+        in_specs=[anym] * 8,
         out_specs=(vmem, vmem),
         scratch_shapes=[
             pltpu.VMEM((n_steps, n_seq, d_model), bf16),
@@ -171,38 +170,70 @@
             pltpu.VMEM((2 * n_steps, w_q.shape[1] // hd + 1, 128, hd), f32),
             pltpu.VMEM((16, 128), f32),
             pltpu.VMEM((8, 16, 128), f32),
-            dma((N_KB, 4)), dma((7,)), dma((7,)),
+            pltpu.VMEM(g_q.shape, bf16),
+            pltpu.VMEM(g_k.shape, bf16),
+            pltpu.VMEM((2, n_seq // 2), jnp.int32),
+            pltpu.VMEM((1, hd), f32),
+            dma((N_KB, 4)), dma((4,)), dma((7,)), dma((7,)),
         ],
-        compiler_params=pltpu.CompilerParams(collective_id=0, has_side_effects=True, vmem_limit_bytes=48 * MIB),
-    )(x_seq, w_q, w_k, w_v, g_q.reshape(1, -1), g_k.reshape(1, -1), cache_len.reshape(2, n_seq // 2), freq)
-
-
-SEQ_BLK = 16
-SEQ_GRP = 8
-
-
-def attn_kernel(n_heads, n_steps, len_ref, q_ref, kv_ref, k_ref, v_ref, o_ref, ko_ref, vo_ref):
-    n_pos, hd = k_ref.shape[1:]
+        compiler_params=pltpu.CompilerParams(collective_id=0, has_side_effects=True, vmem_limit_bytes=63 * MIB),
+    )(x_seq, w_q, w_k, w_v, g_q, g_k, cache_len.reshape(2, n_seq // 2), freq)
+
+
+SEQ_GRP = 16
+N_RING = 8
+AHEAD = 4
+
+
+def attn_kernel(n_heads, n_steps, len_ref, q_hbm, kv_hbm, k_hbm, v_hbm, o_hbm, ko_hbm, vo_hbm, qb, kvb, kb, vb, ob, in_sem, out_sem):
+    n_seq, n_pos, hd = k_hbm.shape
+    n_grp = n_seq // SEQ_GRP
     fixed = n_pos // 2
     scale = hd ** -0.5
-    base = pl.program_id(0) * SEQ_BLK
     row = lax.broadcasted_iota(jnp.int32, (n_pos - fixed, hd), 0)
     s_step = lax.broadcasted_iota(jnp.int32, (16, n_pos - fixed), 0) // n_heads
     s_last = lax.broadcasted_iota(jnp.int32, (16, n_pos - fixed), 1) + fixed - s_step
 
+    def copies(grp, pairs, sem):
+        seqs = pl.ds(grp * SEQ_GRP, SEQ_GRP)
+        s = lax.rem(grp, N_RING)
+        return [pltpu.make_async_copy(hbm.at[seqs], vmem.at[s], sem.at[s, n]) if sem is in_sem else pltpu.make_async_copy(vmem.at[s], hbm.at[seqs], sem.at[s, n]) for n, (hbm, vmem) in enumerate(pairs)]
+
+    def loads(grp):
+        return copies(grp, ((k_hbm, kb), (v_hbm, vb), (q_hbm, qb), (kv_hbm, kvb)), in_sem)
+
+    def stores(grp):
+        return copies(grp, ((ko_hbm, kb), (vo_hbm, vb), (o_hbm, ob)), out_sem)
+
+    for grp in range(AHEAD):
+        for cp in loads(grp):
+            cp.start()
+
     def group(grp, _):
-        first = grp * SEQ_GRP
-        idx = [first + i for i in range(SEQ_GRP)]
-        lens = [len_ref[base + i] for i in idx]
+        slot = lax.rem(grp, N_RING)
+
+        @pl.when(grp + AHEAD < n_grp)
+        def _():
+            @pl.when(grp + AHEAD >= N_RING)
+            def _():
+                for cp in stores(grp + AHEAD - N_RING):
+                    cp.wait()
+
+            for cp in loads(grp + AHEAD):
+                cp.start()
+
+        for cp in loads(grp):
+            cp.wait()
+        idx = range(SEQ_GRP)
+        lens = [len_ref[grp * SEQ_GRP + i] for i in idx]
         for i, length in zip(idx, lens):
             rel = row - (length - fixed)
-            for in_ref, out_ref, slot in ((k_ref, ko_ref, 0), (v_ref, vo_ref, n_steps)):
-                out_ref[i, 0:fixed, :] = in_ref[i, 0:fixed, :]
-                vals = in_ref[i, fixed:n_pos, :].astype(jnp.float32)
+            for buf, first in ((kb, 0), (vb, n_steps)):
+                vals = buf[slot, i, fixed:n_pos, :].astype(jnp.float32)
                 for t in range(n_steps):
-                    vals = jnp.where(rel == t, kv_ref[i, slot + t:slot + t + 1, :], vals)
-                out_ref[i, fixed:n_pos, :] = vals.astype(jnp.bfloat16)
-        scores = [lax.dot_general(q_ref[i].astype(jnp.bfloat16), ko_ref[i], (((1,), (1,)), ((), ())), preferred_element_type=jnp.float32) for i in idx]
+                    vals = jnp.where(rel == t, kvb[slot, i, first + t:first + t + 1, :], vals)
+                buf[slot, i, fixed:n_pos, :] = vals.astype(jnp.bfloat16)
+        scores = [lax.dot_general(qb[slot, i].astype(jnp.bfloat16), kb[slot, i], (((1,), (1,)), ((), ())), preferred_element_type=jnp.float32) for i in idx]
         probs = []
         sums = []
         for s, length in zip(scores, lens):
@@ -214,23 +245,41 @@
             sums.append(jnp.sum(lo + hi, axis=-1, keepdims=True))
             probs.append(jnp.concatenate([lo.astype(jnp.bfloat16), hi.astype(jnp.bfloat16)], axis=-1))
         for i, p, total in zip(idx, probs, sums):
-            o_ref[i] = jnp.dot(p, vo_ref[i], preferred_element_type=jnp.float32) / total
+            ob[slot, i] = jnp.dot(p, vb[slot, i], preferred_element_type=jnp.float32) / total
+        for cp in stores(grp):
+            cp.start()
         return 0
 
-    lax.fori_loop(0, SEQ_BLK // SEQ_GRP, group, 0)
+    lax.fori_loop(0, n_grp, group, 0)
+
+    def drain(grp, _):
+        for cp in stores(grp):
+            cp.wait()
+        return 0
+
+    lax.fori_loop(n_grp - N_RING, n_grp, drain, 0)
 
 
 def attn_layer(cache_len, q, kv, k_cache, v_cache, n_heads, n_steps):
     n_seq, _, n_pos, hd = k_cache.shape
     bf16, f32 = jnp.bfloat16, jnp.float32
-    cache_blk = pl.BlockSpec((SEQ_BLK, n_pos, hd), lambda i: (i, 0, 0))
+    anym = pl.BlockSpec(memory_space=pl.ANY)
+    dma = pltpu.SemaphoreType.DMA
+    ring = (N_RING, SEQ_GRP)
     o, k_out, v_out = pl.pallas_call(
         functools.partial(attn_kernel, n_heads, n_steps),
-        grid=(n_seq // SEQ_BLK,),
         out_shape=(jax.ShapeDtypeStruct((n_seq, 16, hd), f32), jax.ShapeDtypeStruct((n_seq, n_pos, hd), bf16), jax.ShapeDtypeStruct((n_seq, n_pos, hd), bf16)),
-        in_specs=[pl.BlockSpec(memory_space=pltpu.SMEM), pl.BlockSpec((SEQ_BLK, 16, hd), lambda i: (i, 0, 0)), pl.BlockSpec((SEQ_BLK, 8, hd), lambda i: (i, 0, 0)), cache_blk, cache_blk],
-        out_specs=(pl.BlockSpec((SEQ_BLK, 16, hd), lambda i: (i, 0, 0)), cache_blk, cache_blk),
-        compiler_params=pltpu.CompilerParams(vmem_limit_bytes=48 * MIB),
+        in_specs=[pl.BlockSpec(memory_space=pltpu.SMEM)] + [anym] * 4,
+        out_specs=(anym, anym, anym),
+        scratch_shapes=[
+            pltpu.VMEM(ring + (16, hd), f32),
+            pltpu.VMEM(ring + (8, hd), f32),
+            pltpu.VMEM(ring + (n_pos, hd), bf16),
+            pltpu.VMEM(ring + (n_pos, hd), bf16),
+            pltpu.VMEM(ring + (16, hd), f32),
+            dma((N_RING, 4)), dma((N_RING, 3)),
+        ],
+        compiler_params=pltpu.CompilerParams(vmem_limit_bytes=63 * MIB),
     )(cache_len, q.reshape(n_seq, 16, hd), kv.reshape(n_seq, 8, hd), k_cache.reshape(n_seq, n_pos, hd), v_cache.reshape(n_seq, n_pos, hd))
     return o, k_out.reshape(k_cache.shape), v_out.reshape(v_cache.shape)
 
@@ -243,8 +292,8 @@
 DB = 512
 
 
-def tail_kernel(axis, o_hbm, x_hbm, wo_hbm, w1_hbm, w3_hbm, w2_hbm, gains_hbm, y_hbm,
-                on, ob, xp, hb, src, recv0, recv1, recv2, act, wob, wb, w2b, gains,
+def tail_kernel(axis, o_hbm, x_hbm, wo_hbm, w1_hbm, w3_hbm, w2_hbm, ga_hbm, gm_hbm, y_hbm,
+                on, ob, xp, hb, src, recv0, recv1, recv2, act, wob, wb, w2b, ga_ref, gm_ref,
                 o_sem, x_sem, wo_sem, wb_sem, w2_sem, y_sem, gain_sem, s_sem, r_sem, g_ssem, g_rsem):
     n_steps, n_seq, d_model = x_hbm.shape
     piece = n_seq // 8
@@ -281,8 +330,9 @@
 
     for cb in range(N_CB):
         wo_copy(cb).start()
-    gain_copy = pltpu.make_async_copy(gains_hbm, gains, gain_sem)
-    gain_copy.start()
+    gain_copies = (pltpu.make_async_copy(ga_hbm, ga_ref, gain_sem.at[0]), pltpu.make_async_copy(gm_hbm, gm_ref, gain_sem.at[1]))
+    for cp in gain_copies:
+        cp.start()
     x_copy = pltpu.make_async_copy(x_hbm.at[:, pl.ds(pl.multiple_of(piece * me, piece), piece), :], xp, x_sem)
     x_copy.start()
 
@@ -381,7 +431,7 @@
         a = f32(recv2[c, r, :])
         factor = rms_factor(jnp.sum(a * a, axis=-1, keepdims=True), d_model)
         base = f32(xp[c, r, :]) if attn else f32(hb[c, hr, :])
-        gain = gains[0:1, :] if attn else gains[1:2, :]
+        gain = f32((ga_ref if attn else gm_ref)[...]).reshape(1, d_model)
         hb[c, hr, :] = (base + a * factor * gain).astype(jnp.bfloat16)
         for k in (1, 0, 2):
             gcopy(inst, k, sub).start()
@@ -439,7 +489,8 @@
     out_proj(1)
     out_proj(2)
     x_copy.wait()
-    gain_copy.wait()
+    for cp in gain_copies:
+        cp.wait()
 
     def finish_reduce(inst):
         def step(k):
@@ -541,11 +592,10 @@
     bf16 = jnp.bfloat16
     anym = pl.BlockSpec(memory_space=pl.ANY)
     dma = pltpu.SemaphoreType.DMA
-    gains = jnp.stack([g_attn, g_mlp]).astype(jnp.float32)
     return pl.pallas_call(
         functools.partial(tail_kernel, axis),
         out_shape=jax.ShapeDtypeStruct((n_steps, n_seq, d_model), bf16),
-        in_specs=[anym] * 7,
+        in_specs=[anym] * 8,
         out_specs=anym,
         scratch_shapes=[
             pltpu.VMEM(o.shape, jnp.float32),
@@ -560,12 +610,13 @@
             pltpu.VMEM(w_o.shape, bf16),
             pltpu.VMEM((N_WB, d_model, 2 * HB), bf16),
             pltpu.VMEM((N_DB, n_hid, DB), bf16),
-            pltpu.VMEM((2, d_model), jnp.float32),
-            dma, dma, dma((N_CB,)), dma((N_WB, 2)), dma((N_DB,)), dma((n_steps,)), dma,
+            pltpu.VMEM((d_model,), bf16),
+            pltpu.VMEM((d_model,), bf16),
+            dma, dma, dma((N_CB,)), dma((N_WB, 2)), dma((N_DB,)), dma((n_steps,)), dma((2,)),
             dma((2 * n_steps, 4, N_CB)), dma((2 * n_steps, 4, N_CB)), dma((2 * n_steps, 7, N_SUB)), dma((2 * n_steps, 7, N_SUB)),
         ],
         compiler_params=pltpu.CompilerParams(collective_id=1, has_side_effects=True, vmem_limit_bytes=63 * MIB),
-    )(o, x_seq, w_o, w_gate, w_up, w_down, gains)
+    )(o, x_seq, w_o, w_gate, w_up, w_down, g_attn, g_mlp)
 
 
 def layer_steps(x_seq, cache_len, k_cache, v_cache, w_q, w_k, w_v, w_o, w_gate, w_up, w_down, g_q, g_k, g_attn, g_mlp, q_width, kv_width):

time: 271 us -> 254 us (0.937)
  Pallas kernels: 255 us -> 246 us
  local copies, waits for them, and re-layouts: 14.4 us -> 6.98 us
    pallas_call x1, Pallas kernels: 33 us -> 25.4 us  [attn_layer(): pl.pallas_call(functools.partial(attn_kernel, n_heads, n_steps), out_shap...]
    unnamed x11 -> x1, local copies, waits for them, and re-layouts: 12.3 us -> 6.98 us
where the time goes in v2:
time: 254 us
  Pallas kernels  246 us (97%)
  local copies, waits for them, and re-layouts  6.98 us (3%)
    pallas_call x1, Pallas kernels, tail_layer(): pl.pallas_call(functools.partial(tail_kernel, axis), out_shape=jax.ShapeD...  199 us
    pallas_call x1, Pallas kernels, attn_layer(): pl.pallas_call(functools.partial(attn_kernel, n_heads, n_steps), out_shap...  25.4 us
    pallas_call x1, Pallas kernels, head_layer(): pl.pallas_call(functools.partial(head_kernel, axis, q_width, kv_width), o...  21.5 us
    unnamed x1, local copies, waits for them, and re-layouts  6.98 us

profile of v2, /device:TPU:0, one launch (start us, length us, event | category | flops | bytes accessed | tf_op | source)
XLA Modules:
  0.0 254.3 jit_solution(1495081915688252864)
XLA Ops:
  0.6 0.6 maximum_bitcast_fusion.freq_hbm
  1.2 21.5 %shard_map.166 = (f32[4096,128]{1,0:T(8,128)}, f32[2048,128]{1,0:T(8,128)}) custom-call(bf16[3,256,5120]{2,1,0:T(8,128)(2,1)} %x_hbm.3, bf16[5120,640]{1,0:T(8,128)(2,1)} %wq_hbm.1, bf16[5120,128]{1,0:T(8,128)(2,1)} %wk_hbm.1, bf16[5120,128]{1,0:T(8,128)(2,1)} %wv_hbm.1, bf16[640]{0:T(1024)(128)(2,1)} %gq_hbm.1, bf16[128]{0:T(256)(128)(2,1)} %gk_hbm.1, ...), custom_call_target="tpu_custom_call" | custom-call | tf_op jit(solution)/shard_map/pallas_call | solution.py:161
  22.7 25.4 %shard_map.167 = (f32[256,16,128]{2,1,0:T(8,128)}, bf16[256,256,128]{2,1,0:T(8,128)(2,1)}, bf16[256,256,128]{2,1,0:T(8,128)(2,1)}) custom-call(s32[256]{0:T(256)} %len_ref.1, f32[256,16,128]{2,1,0:T(8,128)} %bitcast.17, f32[256,8,128]{2,1,0:T(8,128)} %bitcast.18, bf16[256,256,128]{2,1,0:T(8,128)(2,1)} %bitcast.14, bf16[256,256,128]{2,1,0:T(8,128)(2,1)} %bitcast.15), custom_call_target="tpu_custom_call" | custom-call | tf_op jit(solution)/shard_map/pallas_call | solution.py:269
  48.1 199.3 %shard_map.168 = bf16[3,256,5120]{2,1,0:T(8,128)(2,1)} custom-call(f32[4096,128]{1,0:T(8,128)} %bitcast.16, bf16[3,256,5120]{2,1,0:T(8,128)(2,1)} %x_hbm.3, bf16[640,5120]{1,0:T(8,128)(2,1)} %wo_hbm.1, bf16[5120,3456]{1,0:T(8,128)(2,1)} %w1_hbm.1, bf16[5120,3456]{1,0:T(8,128)(2,1)} %w3_hbm.1, bf16[3456,5120]{1,0:T(8,128)(2,1)} %w2_hbm.1, ...), custom_call_target="tpu_custom_call" | custom-call | tf_op jit(solution)/shard_map/pallas_call | solution.py:595
  247.4 7.0 %copy.21 = bf16[3,256,5120]{2,1,0:T(8,128)(2,1)} copy(bf16[3,256,5120]{2,1,0:T(8,128)(2,1)} %shard_map.168) | data formatting | bytes 15728640
  (1 shorter events, 0.0 us)

commit v3 on v2

--- a/solution.py
+++ b/solution.py
@@ -292,9 +292,9 @@
 DB = 512
 
 
-def tail_kernel(axis, o_hbm, x_hbm, wo_hbm, w1_hbm, w3_hbm, w2_hbm, ga_hbm, gm_hbm, y_hbm,
+def tail_kernel(axis, o_hbm, x_hbm, wo_hbm, w1_hbm, w3_hbm, w2_hbm, ga_hbm, gm_hbm, y_ref,
                 on, ob, xp, hb, src, recv0, recv1, recv2, act, wob, wb, w2b, ga_ref, gm_ref,
-                o_sem, x_sem, wo_sem, wb_sem, w2_sem, y_sem, gain_sem, s_sem, r_sem, g_ssem, g_rsem):
+                o_sem, x_sem, wo_sem, wb_sem, w2_sem, gain_sem, s_sem, r_sem, g_ssem, g_rsem):
     n_steps, n_seq, d_model = x_hbm.shape
     piece = n_seq // 8
     sub_rows = piece // N_SUB
@@ -326,7 +326,8 @@
     o_copy.start()
 
     def wo_copy(cb):
-        return pltpu.make_async_copy(wo_hbm.at[:, pl.ds(cb * cw, cw)], wob.at[:, pl.ds(cb * cw, cw)], wo_sem.at[cb])
+        cols = pl.ds(pl.multiple_of(cb * cw, cw), cw)
+        return pltpu.make_async_copy(wo_hbm.at[:, cols], wob.at[:, cols], wo_sem.at[cb])
 
     for cb in range(N_CB):
         wo_copy(cb).start()
@@ -349,8 +350,6 @@
             for cp in wb_copies(s, s):
                 cp.start()
 
-    start_wb()
-
     bar = pltpu.get_barrier_semaphore()
     for dev in (partner, fpeer, speer):
         pl.semaphore_signal(bar, inc=1, device_id={axis: dev}, device_id_type=MESH_ID)
@@ -382,7 +381,7 @@
         cols = cols_of(cb)
 
         def add(i, _):
-            recv0[c, i, :, cols] = (f32(src[c, i, core, :, cols]) + f32(recv0[c, i, :, cols])).astype(jnp.bfloat16)
+            recv0[c, i, :, cols] = src[c, i, core, :, cols] + recv0[c, i, :, cols]
             return 0
 
         lax.fori_loop(0, 4, add, 0)
@@ -394,7 +393,7 @@
         copy1(inst, cb, 0).wait_recv()
         cols = cols_of(cb)
         idx = first_bit * fw + (1 - second_bit) * sw
-        recv1[c, 0, :, cols] = (f32(recv0[c, idx, :, cols]) + f32(recv1[c, 0, :, cols])).astype(jnp.bfloat16)
+        recv1[c, 0, :, cols] = recv0[c, idx, :, cols] + recv1[c, 0, :, cols]
         copy2(inst, cb).start()
 
     def event3(inst, cb):
@@ -472,19 +471,24 @@
             ob[:, g * hd:(g + 1) * hd] = on[pl.ds(c * n_heads + g, n_seq, stride=16), :].astype(jnp.bfloat16)
 
         def step(cb):
+            if c == 0:
+                wo_copy(cb).wait()
             part = jnp.dot(ob[...], wob[:, cols_of(cb)], preferred_element_type=jnp.float32).astype(jnp.bfloat16)
             src[c, :, :, :, cols_of(cb)] = part.reshape(4, 2, piece, cw)
             copy0(c, cb).start()
 
         loop(N_CB, step)
 
-    def y_copy(c):
-        return pltpu.make_async_copy(hb.at[c], y_hbm.at[c], y_sem.at[c])
+    def y_store(c):
+        def step(i):
+            r = pl.ds(pl.multiple_of(i * piece, piece), piece)
+            y_ref[c, r, :] = hb[c, r, :]
+
+        loop(8, step)
 
     o_copy.wait()
-    for cb in range(N_CB):
-        wo_copy(cb).wait()
     out_proj(0)
+    start_wb()
     loop(N_CB, functools.partial(event1, 0))
     out_proj(1)
     out_proj(2)
@@ -570,8 +574,6 @@
             event4(2, 1)
 
     last = 2 * n_steps - 1
-    for c in range(n_steps - 1):
-        y_copy(c).start()
     event1(last, 4)
     event2(last, 3)
     event3(last, 1)
@@ -579,10 +581,13 @@
     event2(last, 4)
     event3(last, 3)
     event3(last, 4)
-    finish_gather(last)
-    y_copy(n_steps - 1).start()
-    for c in range(n_steps):
-        y_copy(c).wait()
+    loop(N_SUB, functools.partial(event4, last))
+    for c in range(n_steps - 1):
+        y_store(c)
+    loop(N_SUB, functools.partial(event5, last))
+    loop(N_SUB, functools.partial(event7, last))
+    loop(N_SUB, functools.partial(event8, last))
+    y_store(n_steps - 1)
 
 
 def tail_layer(o, x_seq, w_o, w_gate, w_up, w_down, g_attn, g_mlp, axis):
@@ -594,9 +599,9 @@
     dma = pltpu.SemaphoreType.DMA
     return pl.pallas_call(
         functools.partial(tail_kernel, axis),
-        out_shape=jax.ShapeDtypeStruct((n_steps, n_seq, d_model), bf16),
+        out_shape=pltpu.VMEM((n_steps, n_seq, d_model), bf16),
         in_specs=[anym] * 8,
-        out_specs=anym,
+        out_specs=pl.BlockSpec(memory_space=pltpu.VMEM),
         scratch_shapes=[
             pltpu.VMEM(o.shape, jnp.float32),
             pltpu.VMEM((n_seq, w_o.shape[0]), bf16),
@@ -612,10 +617,10 @@
             pltpu.VMEM((N_DB, n_hid, DB), bf16),
             pltpu.VMEM((d_model,), bf16),
             pltpu.VMEM((d_model,), bf16),
-            dma, dma, dma((N_CB,)), dma((N_WB, 2)), dma((N_DB,)), dma((n_steps,)), dma((2,)),
+            dma, dma, dma((N_CB,)), dma((N_WB, 2)), dma((N_DB,)), dma((2,)),
             dma((2 * n_steps, 4, N_CB)), dma((2 * n_steps, 4, N_CB)), dma((2 * n_steps, 7, N_SUB)), dma((2 * n_steps, 7, N_SUB)),
         ],
-        compiler_params=pltpu.CompilerParams(collective_id=1, has_side_effects=True, vmem_limit_bytes=63 * MIB),
+        compiler_params=pltpu.CompilerParams(collective_id=1, has_side_effects=True, vmem_limit_bytes=55 * MIB),
     )(o, x_seq, w_o, w_gate, w_up, w_down, g_attn, g_mlp)
 
 

time: 254 us -> 247 us (0.972)
  Pallas kernels: 246 us -> 242 us
  local copies, waits for them, and re-layouts: 6.98 us -> 3.22 us
    pallas_call x1, Pallas kernels: 199 us -> 195 us  [tail_layer(): pl.pallas_call(functools.partial(tail_kernel, axis), out_shape=pltpu.VMEM...]
    unnamed x1, local copies, waits for them, and re-layouts: 6.98 us -> 3.22 us
where the time goes in v3:
time: 247 us; the launch traced here: 246 us
  Pallas kernels  242 us (98%)
  local copies, waits for them, and re-layouts  3.22 us (1%)
    pallas_call x1, Pallas kernels, tail_layer(): pl.pallas_call(functools.partial(tail_kernel, axis), out_shape=pltpu.VMEM...  195 us
    pallas_call x1, Pallas kernels, attn_layer(): pl.pallas_call(functools.partial(attn_kernel, n_heads, n_steps), out_shap...  25.4 us
    pallas_call x1, Pallas kernels, head_layer(): pl.pallas_call(functools.partial(head_kernel, axis, q_width, kv_width), o...  21.5 us

profile of v3, /device:TPU:0, one launch (start us, length us, event | category | flops | bytes accessed | tf_op | source)
XLA Modules:
  0.0 246.5 jit_solution(17797198025096957103)
XLA Ops:
  0.6 0.6 maximum_bitcast_fusion.freq_hbm
  1.2 21.5 %shard_map.166 = (f32[4096,128]{1,0:T(8,128)}, f32[2048,128]{1,0:T(8,128)}) custom-call(bf16[3,256,5120]{2,1,0:T(8,128)(2,1)} %x_hbm.3, bf16[5120,640]{1,0:T(8,128)(2,1)} %wq_hbm.1, bf16[5120,128]{1,0:T(8,128)(2,1)} %wk_hbm.1, bf16[5120,128]{1,0:T(8,128)(2,1)} %wv_hbm.1, bf16[640]{0:T(1024)(128)(2,1)} %gq_hbm.1, bf16[128]{0:T(256)(128)(2,1)} %gk_hbm.1, ...), custom_call_target="tpu_custom_call" | custom-call | tf_op jit(solution)/shard_map/pallas_call | solution.py:161
  22.7 25.4 %shard_map.167 = (f32[256,16,128]{2,1,0:T(8,128)}, bf16[256,256,128]{2,1,0:T(8,128)(2,1)}, bf16[256,256,128]{2,1,0:T(8,128)(2,1)}) custom-call(s32[256]{0:T(256)} %len_ref.1, f32[256,16,128]{2,1,0:T(8,128)} %bitcast.17, f32[256,8,128]{2,1,0:T(8,128)} %bitcast.18, bf16[256,256,128]{2,1,0:T(8,128)(2,1)} %bitcast.14, bf16[256,256,128]{2,1,0:T(8,128)(2,1)} %bitcast.15), custom_call_target="tpu_custom_call" | custom-call | tf_op jit(solution)/shard_map/pallas_call | solution.py:269
  48.1 195.1 %shard_map.168 = bf16[3,256,5120]{2,1,0:T(8,128)(2,1)S(1)} custom-call(f32[4096,128]{1,0:T(8,128)} %bitcast.16, bf16[3,256,5120]{2,1,0:T(8,128)(2,1)} %x_hbm.3, bf16[640,5120]{1,0:T(8,128)(2,1)} %wo_hbm.1, bf16[5120,3456]{1,0:T(8,128)(2,1)} %w1_hbm.1, bf16[5120,3456]{1,0:T(8,128)(2,1)} %w3_hbm.1, bf16[3456,5120]{1,0:T(8,128)(2,1)} %w2_hbm.1, ...), custom_call_target="tpu_custom_call" | custom-call | tf_op jit(solution)/shard_map/pallas_call | solution.py:600
  243.3 3.2 %copy.21 = bf16[3,256,5120]{2,1,0:T(8,128)(2,1)} copy(bf16[3,256,5120]{2,1,0:T(8,128)(2,1)S(1)} %shard_map.168) | data formatting | bytes 15728640
  (1 shorter events, 0.0 us)

commit v4 on v3

--- a/solution.py
+++ b/solution.py
@@ -2,6 +2,7 @@
 
 import jax
 import jax.numpy as jnp
+import numpy as np
 from jax import lax
 from jax.experimental import pallas as pl
 from jax.experimental.pallas import tpu as pltpu
@@ -153,8 +154,8 @@
     cols = w_q.shape[1] + 2 * hd
     half_dim = hd // 2
     bf16, f32 = jnp.bfloat16, jnp.float32
-    inv_freq = ROPE_THETA ** (-(jnp.arange(half_dim, dtype=f32) * (2.0 / hd)))
-    freq = jnp.concatenate([inv_freq, inv_freq]).reshape(1, hd)
+    inv_freq = ROPE_THETA ** (-(np.arange(half_dim) * (2.0 / hd)))
+    freq = jnp.asarray(np.concatenate([inv_freq, inv_freq]).reshape(1, hd), dtype=f32)
     anym = pl.BlockSpec(memory_space=pl.ANY)
     vmem = pl.BlockSpec(memory_space=pltpu.VMEM)
     dma = pltpu.SemaphoreType.DMA
@@ -491,7 +492,6 @@
     start_wb()
     loop(N_CB, functools.partial(event1, 0))
     out_proj(1)
-    out_proj(2)
     x_copy.wait()
     for cp in gain_copies:
         cp.wait()
@@ -508,14 +508,12 @@
 
         loop(N_CB + 1, step)
 
-    def finish_gather(inst):
-        loop(N_SUB, functools.partial(event4, inst))
-        loop(N_SUB, functools.partial(event5, inst))
-        loop(N_SUB, functools.partial(event7, inst))
-        loop(N_SUB, functools.partial(event8, inst))
-
     finish_reduce(0)
-    finish_gather(0)
+    loop(N_SUB, functools.partial(event4, 0))
+    out_proj(2)
+    loop(N_SUB, functools.partial(event5, 0))
+    loop(N_SUB, functools.partial(event7, 0))
+    loop(N_SUB, functools.partial(event8, 0))
 
     gate_tables = (
         ((event1, 1, 0, 1, N_CB), (event2, 1, 4, 2, N_CB), (event3, 1, 9, 2, N_CB), (event4, 1, 18, 1, N_SUB), (event1, 2, 20, 1, N_CB)),

time: 247 us -> 243 us (0.984)
  Pallas kernels: 242 us -> 239 us
    pallas_call x1, Pallas kernels: 195 us -> 193 us  [tail_layer(): pl.pallas_call(functools.partial(tail_kernel, axis), out_shape=pltpu.VMEM...]
where the time goes in v4:
time: 243 us
  Pallas kernels  239 us (98%)
  local copies, waits for them, and re-layouts  3.22 us (1%)
    pallas_call x1, Pallas kernels, tail_layer(): pl.pallas_call(functools.partial(tail_kernel, axis), out_shape=pltpu.VMEM...  193 us
    pallas_call x1, Pallas kernels, attn_layer(): pl.pallas_call(functools.partial(attn_kernel, n_heads, n_steps), out_shap...  25.4 us
    pallas_call x1, Pallas kernels, head_layer(): pl.pallas_call(functools.partial(head_kernel, axis, q_width, kv_width), o...  21.5 us

profile of v4, /device:TPU:0, one launch (start us, length us, event | category | flops | bytes accessed | tf_op | source)
XLA Modules:
  0.0 243.3 jit_solution(8253609466694387334)
XLA Ops:
  0.6 21.5 %shard_map.175 = (f32[4096,128]{1,0:T(8,128)}, f32[2048,128]{1,0:T(8,128)}) custom-call(bf16[3,256,5120]{2,1,0:T(8,128)(2,1)} %x_hbm.3, bf16[5120,640]{1,0:T(8,128)(2,1)} %wq_hbm.1, bf16[5120,128]{1,0:T(8,128)(2,1)} %wk_hbm.1, bf16[5120,128]{1,0:T(8,128)(2,1)} %wv_hbm.1, bf16[640]{0:T(1024)(128)(2,1)} %gq_hbm.1, bf16[128]{0:T(256)(128)(2,1)} %gk_hbm.1, ...), custom_call_target="tpu_custom_call" | custom-call | tf_op jit(solution)/shard_map/pallas_call | solution.py:162
  22.1 25.4 %shard_map.176 = (f32[256,16,128]{2,1,0:T(8,128)}, bf16[256,256,128]{2,1,0:T(8,128)(2,1)}, bf16[256,256,128]{2,1,0:T(8,128)(2,1)}) custom-call(s32[256]{0:T(256)} %len_ref.1, f32[256,16,128]{2,1,0:T(8,128)} %bitcast.15, f32[256,8,128]{2,1,0:T(8,128)} %bitcast.16, bf16[256,256,128]{2,1,0:T(8,128)(2,1)} %bitcast.12, bf16[256,256,128]{2,1,0:T(8,128)(2,1)} %bitcast.13), custom_call_target="tpu_custom_call" | custom-call | tf_op jit(solution)/shard_map/pallas_call | solution.py:270
  47.5 192.6 %shard_map.177 = bf16[3,256,5120]{2,1,0:T(8,128)(2,1)S(1)} custom-call(f32[4096,128]{1,0:T(8,128)} %bitcast.14, bf16[3,256,5120]{2,1,0:T(8,128)(2,1)} %x_hbm.3, bf16[640,5120]{1,0:T(8,128)(2,1)} %wo_hbm.1, bf16[5120,3456]{1,0:T(8,128)(2,1)} %w1_hbm.1, bf16[5120,3456]{1,0:T(8,128)(2,1)} %w3_hbm.1, bf16[3456,5120]{1,0:T(8,128)(2,1)} %w2_hbm.1, ...), custom_call_target="tpu_custom_call" | custom-call | tf_op jit(solution)/shard_map/pallas_call | solution.py:598
  240.1 3.2 %copy.22 = bf16[3,256,5120]{2,1,0:T(8,128)(2,1)} copy(bf16[3,256,5120]{2,1,0:T(8,128)(2,1)S(1)} %shard_map.177) | data formatting | bytes 15728640
